TPU v7x, 512 devices: a whole 4x4x16 slice. The times are simulated.
512 devices in a mesh: dp: 64 (over z, y), tensor: 8 (over x, core).
Axes of the slice: x: 4, y: 4, z: 16, core: 2. Of those that a mesh axis runs over, the one named last changes fastest.
Arguments:
- layer_input: bfloat16 [8192, 8192], P('dp', 'tensor'), may hold values from -6 to 6
- output_grad: bfloat16 [8192, 8192], P('dp', 'tensor'), may hold values from -0.06591797 to 0.06591797
- gate_pre: bfloat16 [8192, 28672], P('dp', 'tensor'), may hold values from -6 to 6
- up_pre: bfloat16 [8192, 28672], P('dp', 'tensor'), may hold values from -6 to 6
- hidden_grad: bfloat16 [8192, 28672], P('dp', 'tensor'), may hold values from -0.06591797 to 0.06591797
- tile_list: int32 [448, 3], P('tensor'), may hold values from 0 to 63, as said below
- tile_slots: int32 [448], P('tensor'), may hold values from 0 to 127, as said below
- first_codes: int32 [8, 128, 16384], P('tensor', 'dp'), may hold values from 0 to 255
- second_codes: int32 [8, 128, 16384], P('tensor', 'dp'), may hold values from 0 to 255
- first_absmax: float32 [8, 128, 8], P('tensor', 'dp'), may hold values from 0.05 to 0.5
- second_absmax: float32 [8, 128, 8], P('tensor', 'dp'), may hold values from 0.005 to 0.05
- signed_map: float32 [256], replicated, may hold values from -1 to 1
- unsigned_map: float32 [256], replicated, may hold values from 0.05 to 1
Outputs:
- update_tiles: bfloat16 [448, 128, 128], P('tensor')
- first_moment: float32 [8, 128, 16384], P('tensor', 'dp')
- second_moment: float32 [8, 128, 16384], P('tensor', 'dp')
Inputs may be any that keep to these rules, and one draw needn't show every extreme that they name: `tile_list`: within each group of 56 rows that belongs to one tensor index the triples are distinct; the first entry is below 64, the second below 28, the third is 0, 1 or 2. `tile_slots`: within each group of 56 entries the slots are distinct; a dp index owns slots s with s // 2 equal to it, so it holds at most 2 tiles of a group, and in every group some dp index holds exactly 2.
All inputs are finite; a program needn't handle non-finite values.
Results may differ from a plain program's by a relative error of at most 0.0085.
Values may be sent and summed in bfloat16 or wider, within the bound.
A program may use at most 64 MiB of HBM per device.

v0:
```python
import jax
import jax.numpy as jnp
from jax import lax
from jax.sharding import PartitionSpec as P

CAP = 2
TB = 128
STEP = 10
BETA_FIRST = 0.9
BETA_SECOND = 0.99
EPSILON = 1e-08


def lookup(code_table, level_table):
    levels = jnp.arange(16, dtype=jnp.int32)
    high_part = jnp.right_shift(code_table, 4)
    low_part = jnp.bitwise_and(code_table, 15)
    low_onehot = (low_part[:, None, :] == levels[None, :, None]).astype(jnp.bfloat16)
    high_onehot = (high_part[:, None, :] == levels[None, :, None]).astype(jnp.float32)
    square = level_table.reshape(16, 16)
    first_part = square.astype(jnp.bfloat16)
    remain = square - first_part.astype(jnp.float32)
    second_part = remain.astype(jnp.bfloat16)
    third_part = (remain - second_part.astype(jnp.float32)).astype(jnp.bfloat16)
    total = jnp.zeros(code_table.shape, jnp.float32)
    for level_part in (third_part, second_part, first_part):
        by_high = jnp.einsum(
            "hl,cln->chn", level_part, low_onehot, preferred_element_type=jnp.float32
        )
        total = total + jnp.sum(by_high * high_onehot, axis=1)
    return total


def dequantize(code_table, level_table, scales):
    values = lookup(code_table, level_table)
    shaped = values.reshape(code_table.shape[0], scales.shape[1], -1) * scales[:, :, None]
    return shaped.reshape(code_table.shape)


def body(
    layer_input,
    output_grad,
    gate_pre,
    up_pre,
    hidden_grad,
    tile_list,
    tile_slots,
    first_codes,
    second_codes,
    first_absmax,
    second_absmax,
    signed_map,
    unsigned_map,
):
    whole_input, whole_grad = (
        lax.all_gather(layer_input, "tensor", axis=1, tiled=True),
        lax.all_gather(output_grad, "tensor", axis=1, tiled=True),
    )
    tokens_here = whole_input.shape[0]
    tile_count = tile_list.shape[0]
    gate_value = gate_pre.astype(jnp.float32)
    up_value = up_pre.astype(jnp.float32)
    grad_value = hidden_grad.astype(jnp.float32)
    sigmoid_gate = jax.nn.sigmoid(gate_value)
    silu_gate = gate_value * sigmoid_gate
    hidden = (silu_gate * up_value).astype(jnp.bfloat16)
    gate_grad = (
        grad_value * up_value * sigmoid_gate * (1.0 + gate_value * (1.0 - sigmoid_gate))
    ).astype(jnp.bfloat16)
    up_grad = (grad_value * silu_gate).astype(jnp.bfloat16)
    width_block = tile_list[:, 0]
    hidden_block = tile_list[:, 1]
    matrix_id = tile_list[:, 2][None, :, None]

    def blocks(source, block_index):
        return jnp.take(source.reshape(tokens_here, -1, TB), block_index, axis=1)

    left_side = jnp.where(
        matrix_id == 2, blocks(hidden, hidden_block), blocks(whole_input, width_block)
    )
    right_side = jnp.where(
        matrix_id == 0,
        blocks(gate_grad, hidden_block),
        jnp.where(matrix_id == 1, blocks(up_grad, hidden_block), blocks(whole_grad, width_block)),
    )
    partial_value = jnp.einsum(
        "tki,tkj->kij", left_side, right_side, preferred_element_type=jnp.float32
    )
    partial_value = partial_value.reshape(tile_count, -1)
    owner_index = lax.axis_index("dp")
    slot_ids = owner_index * CAP + jnp.arange(CAP, dtype=jnp.int32)
    summed = lax.psum(partial_value, "dp")
    slot_match = (tile_slots[None, :] == slot_ids[:, None]).astype(jnp.float32)
    own_grad = jnp.dot(slot_match, summed, precision=lax.Precision.HIGHEST)
    first_old = dequantize(first_codes[0], signed_map, first_absmax[0])
    second_old = dequantize(second_codes[0], unsigned_map, second_absmax[0])
    first_moment = BETA_FIRST * first_old + (1.0 - BETA_FIRST) * own_grad
    second_moment = BETA_SECOND * second_old + (1.0 - BETA_SECOND) * own_grad * own_grad
    first_hat = first_moment / (1.0 - BETA_FIRST**STEP)
    second_hat = second_moment / (1.0 - BETA_SECOND**STEP)
    slot_update = (first_hat / (jnp.sqrt(second_hat) + EPSILON)).astype(jnp.bfloat16)
    everyone = lax.all_gather(slot_update, "dp", axis=0, tiled=True)
    picked = jnp.take(everyone, tile_slots, axis=0)
    return (picked.reshape(tile_count, TB, TB), first_moment[None], second_moment[None])


def solution(mesh):
    in_specs = (
        P("dp", "tensor"),
        P("dp", "tensor"),
        P("dp", "tensor"),
        P("dp", "tensor"),
        P("dp", "tensor"),
        P("tensor", None),
        P("tensor"),
        P("tensor", "dp", None),
        P("tensor", "dp", None),
        P("tensor", "dp", None),
        P("tensor", "dp", None),
        P(),
        P(),
    )
    out_specs = (P("tensor", None, None), P("tensor", "dp", None), P("tensor", "dp", None))
    return jax.shard_map(body, mesh=mesh, in_specs=in_specs, out_specs=out_specs, check_vma=False)
```

profile of v0, /device:TPU:2, one launch (start us, length us, event | category | flops | bytes accessed | tf_op | source)
XLA Modules:
  0.0 557.6 jit_solution(2680922352320135020)
XLA Ops:
  7.2 1.9 copy.42
  9.2 1.8 copy.37
  11.1 0.8 compare_and_fusion.1
  12.5 1.3 copy.35
  13.8 1.3 copy.39
  15.1 3.5 fusion.6
  19.2 1.6 copy.40
  20.8 2.2 gather_fusion.1
  23.0 2.0 gather_fusion.3
  25.7 2.1 gather_fusion.4
  28.5 0.9 fusion.36
  29.4 0.7 compare_bitcast_fusion.2
  30.0 16.4 %all-gather.7.cloned.1.call-done = bf16[128,8192]{0,1:T(8,128)(2,1)} async-done(((bf16[128,1024]{0,1:T(8,128)(2,1)}), bf16[128,8192]{0,1:T(8,128)(2,1)}) %all-gather.7.cloned.1.call-update) | async-done | bytes 2097168 | tf_op jit(solution)/shard_map/all_gather | solution.py:57
  46.4 3.2 copy.43
  49.7 32.4 %all-gather.5.cloned.1.call-done = bf16[128,8192]{0,1:T(8,128)(2,1)} async-done(((bf16[128,1024]{0,1:T(8,128)(2,1)}), bf16[128,8192]{0,1:T(8,128)(2,1)}) %all-gather.5.cloned.1.call-update) | async-done | bytes 2097168 | tf_op jit(solution)/shard_map/all_gather | solution.py:56
  82.0 4.1 copy.38
  86.1 2.0 gather_fusion.5
  88.1 3.8 gather_fusion.2
  91.9 4.2 fusion.16
  96.1 3.9 copy.51
  100.3 0.6 copy-done.6
  101.0 0.9 fusion.33
  101.9 0.9 fusion.32
  102.8 0.9 fusion.35
  103.7 0.9 fusion.31
  104.6 0.9 fusion.34
  105.5 284.1 %all-reduce.2.cloned.1.call-done = f32[56,16384]{1,0:T(8,128)} async-done(((f32[56,16384]{1,0:T(8,128)}), f32[56,16384]{1,0:T(8,128)}) %all-reduce.2.cloned.1.call-update) | async-done | bytes 3670032 | tf_op jit(solution)/shard_map/psum | solution.py:92
  389.6 4.4 fusion.46
  394.1 141.6 %all-gather.9.cloned.1.call-done = bf16[64,2,16384]{2,1,0:T(2,128)(2,1)} async-done(((bf16[1,2,16384]{2,1,0:T(2,128)(2,1)}), bf16[64,2,16384]{2,1,0:T(2,128)(2,1)}) %all-gather.9.cloned.1.call-update) | async-done | bytes 4194320 | tf_op jit(solution)/shard_map/all_gather | solution.py:102
  535.7 7.2 %reshape.189 = bf16[128,16384]{1,0:T(8,128)(2,1)} reshape(bf16[64,2,16384]{2,1,0:T(2,128)(2,1)} %all-gather.9.cloned.1.call-done) | data formatting | bytes 8388608
  543.0 6.0 %gather_fusion = bf16[56,16384]{1,0:T(8,128)(2,1)S(1)} fusion(bf16[128,16384]{1,0:T(8,128)(2,1)} %reshape.189, s32[1024]{0:T(1024)S(1)} %pad_clamp_fusion), kind=kCustom, calls=%fused_computation.5 | custom fusion | bytes 3670240 | tf_op jit(solution)/shard_map/jit(_take)/gather | solution.py:103
  549.5 1.6 bitcast_select_fusion
  (46 shorter events, 3.6 us)
Async XLA Ops:
  7.2 20.8 %copy-start = (f32[1,2,8]{2,1,0:T(2,128)S(1)}, f32[1,2,8]{2,1,0:T(2,128)}, u32[]{:S(2)}) copy-start(f32[1,2,8]{2,1,0:T(2,128)} %param.26) | copy-start | bytes 196
  7.2 4.7 copy-start.2
  7.2 5.3 copy-start.3
  7.2 39.2 %all-gather.7.cloned.1.call-start = ((), (), s32[]{:S(2)}) async-start(), calls=%async_computation.1 | async-start | bytes 2359296 | tf_op jit(solution)/shard_map/all_gather | solution.py:57
  9.2 72.9 %all-gather.5.cloned.1.call-start = ((), (), s32[]{:S(2)}) async-start(), calls=%async_computation | async-start | bytes 2359296 | tf_op jit(solution)/shard_map/all_gather | solution.py:56
  11.0 378.6 %all-reduce.2.cloned.1.call-start = ((), (), s32[]{:S(2)}) async-start(), calls=%async_computation.2 | async-start | bytes 7340032 | tf_op jit(solution)/shard_map/psum | solution.py:92
  12.5 1.3 copy-start.4
  25.7 2.1 copy-start.8
  25.7 2.2 copy-start.9
  25.7 2.4 copy-start.7
  25.7 2.6 copy-start.5
  88.1 3.8 copy-start.1
  100.0 0.9 copy-start.6
  100.0 435.7 %all-gather.9.cloned.1.call-start = ((), (), s32[]{:S(2)}) async-start(), calls=%async_computation.3 | async-start | bytes 4259840 | tf_op jit(solution)/shard_map/all_gather | solution.py:102
  104.6 285.0 %copy-start.10 = (s32[56]{0:T(128)S(1)}, s32[56]{0:T(128)}, u32[]{:S(2)}) copy-start(s32[56]{0:T(128)} %param.23) | copy-start | bytes 676
Sparse Core Ops, SparseCore 0:
  10.2 36.2 all-gather.6
  48.6 33.4 all-gather.4
  100.2 289.4 all-reduce.1
  394.2 141.4 all-gather.8
where the time goes:
time: 558 us
  waiting for transfers between devices  475 us (85%)
  local copies, waits for them, and re-layouts  47.9 us (9%)
  matrix products  14 us (3%)
  between operations  14 us (3%)
  other arithmetic  6.76 us (1%)
    psum x1, waiting for transfers between devices, body(): summed = lax.psum(partial_value, 'dp')  284 us
    all_gather x1, waiting for transfers between devices, body(): everyone = lax.all_gather(slot_update, 'dp', axis=0, tiled=True)  142 us
    all_gather x1, waiting for transfers between devices, body(): lax.all_gather(layer_input, 'tensor', axis=1, tiled=True)  32.4 us
    unnamed x34, local copies, waits for them, and re-layouts  19.6 us
    all_gather x1, waiting for transfers between devices, body(): lax.all_gather(output_grad, 'tensor', axis=1, tiled=True)  16.4 us
    gather x5, local copies, waits for them, and re-layouts, blocks(): return jnp.take(source.reshape(tokens_here, -1, TB), block_index, axis=1)  12.1 us
  transfers between devices with their start and end apart: 4, of which 4 were waited for; matrix products, arithmetic and copies ran while one was open for 5% of the time, Pallas kernels for 0%

commit v1 on v0

--- a/solution.py
+++ b/solution.py
@@ -2,6 +2,7 @@
 import jax.numpy as jnp
 from jax import lax
 from jax.sharding import PartitionSpec as P
+from jax.lax import all_to_all, axis_size
 
 CAP = 2
 TB = 128
@@ -99,7 +100,10 @@
     first_hat = first_moment / (1.0 - BETA_FIRST**STEP)
     second_hat = second_moment / (1.0 - BETA_SECOND**STEP)
     slot_update = (first_hat / (jnp.sqrt(second_hat) + EPSILON)).astype(jnp.bfloat16)
-    everyone = lax.all_gather(slot_update, "dp", axis=0, tiled=True)
+    found = []
+    for _ in range(axis_size("dp")):
+        found.append(slot_update)
+    everyone = jnp.concatenate(all_to_all(jnp.stack(found), "dp", 0, 0), 0)
     picked = jnp.take(everyone, tile_slots, axis=0)
     return (picked.reshape(tile_count, TB, TB), first_moment[None], second_moment[None])
 

time: 558 us -> 614 us (1.10)
  waiting for transfers between devices: 475 us -> 514 us
  starting transfers between devices: 0.34 us -> 10.1 us
  local copies, waits for them, and re-layouts: 47.9 us -> 54.2 us
    all_to_all x0 -> x1, waiting for transfers between devices: none -> 181 us  [body(): everyone = jnp.concatenate(all_to_all(jnp.stack(found), 'dp', 0, 0), 0)]
    all_gather x1 -> x0, waiting for transfers between devices: 142 us -> none  [body(): everyone = lax.all_gather(slot_update, 'dp', axis=0, tiled=True)]
    all_to_all x0 -> x1, starting transfers between devices: none -> 9.98 us  [body(): everyone = jnp.concatenate(all_to_all(jnp.stack(found), 'dp', 0, 0), 0)]
    reshape x0 -> x1, local copies, waits for them, and re-layouts: none -> 7.26 us  [body(): everyone = jnp.concatenate(all_to_all(jnp.stack(found), 'dp', 0, 0), 0)]
    unnamed x34 -> x33, local copies, waits for them, and re-layouts: 19.6 us -> 12.6 us
where the time goes in v1:
time: 614 us; the launch traced here: 613 us
  waiting for transfers between devices  514 us (84%)
  local copies, waits for them, and re-layouts  54.2 us (9%)
  matrix products  14.2 us (2%)
  between operations  14 us (2%)
  starting transfers between devices  10.1 us (2%)
  other arithmetic  6.76 us (1%)
    psum x1, waiting for transfers between devices, body(): summed = lax.psum(partial_value, 'dp')  284 us
    all_to_all x1, waiting for transfers between devices, body(): everyone = jnp.concatenate(all_to_all(jnp.stack(found), 'dp', 0, 0), 0)  181 us
    all_gather x1, waiting for transfers between devices, body(): lax.all_gather(layer_input, 'tensor', axis=1, tiled=True)  32.4 us
    all_gather x1, waiting for transfers between devices, body(): lax.all_gather(output_grad, 'tensor', axis=1, tiled=True)  16.4 us
    unnamed x33, local copies, waits for them, and re-layouts  12.6 us
  transfers between devices with their start and end apart: 4, of which 4 were waited for; matrix products, arithmetic and copies ran while one was open for 5% of the time, Pallas kernels for 0%

profile of v1, /device:TPU:2, one launch (start us, length us, event | category | flops | bytes accessed | tf_op | source)
XLA Modules:
  0.0 613.2 jit_solution(17938761340227788819)
XLA Ops:
  7.2 1.9 copy.31
  9.2 1.8 copy.26
  12.5 1.3 copy.24
  13.8 1.3 copy.28
  15.1 3.5 fusion.6
  19.3 1.6 copy.29
  20.9 2.1 gather_fusion.1
  23.0 2.0 gather_fusion.3
  25.7 2.1 gather_fusion.4
  28.4 0.9 fusion.36
  30.0 16.4 %all-gather.5.cloned.1.call-done = bf16[128,8192]{0,1:T(8,128)(2,1)} async-done(((bf16[128,1024]{0,1:T(8,128)(2,1)}), bf16[128,8192]{0,1:T(8,128)(2,1)}) %all-gather.5.cloned.1.call-update) | async-done | bytes 2097168 | tf_op jit(solution)/shard_map/all_gather | solution.py:58
  46.4 3.2 copy.32
  49.7 32.4 %all-gather.3.cloned.1.call-done = bf16[128,8192]{0,1:T(8,128)(2,1)} async-done(((bf16[128,1024]{0,1:T(8,128)(2,1)}), bf16[128,8192]{0,1:T(8,128)(2,1)}) %all-gather.3.cloned.1.call-update) | async-done | bytes 2097168 | tf_op jit(solution)/shard_map/all_gather | solution.py:57
  82.0 4.1 copy.27
  86.1 2.0 gather_fusion.5
  88.1 3.8 gather_fusion.2
  91.9 4.4 fusion.16
  96.3 3.9 copy.40
  100.2 0.9 copy-done.6
  101.2 0.9 fusion.33
  102.1 0.9 fusion.32
  103.0 0.9 fusion.35
  103.9 0.9 fusion.31
  104.8 0.9 fusion.34
  105.7 284.1 %all-reduce.2.cloned.1.call-done = f32[56,16384]{1,0:T(8,128)} async-done(((f32[56,16384]{1,0:T(8,128)}), f32[56,16384]{1,0:T(8,128)}) %all-reduce.2.cloned.1.call-update) | async-done | bytes 3670032 | tf_op jit(solution)/shard_map/psum | solution.py:93
  389.7 4.4 fusion.45
  394.2 6.0 stack.2
  400.2 10.0 %all-to-all-start = ((bf16[64,2,16384]{2,1,0:T(2,128)(2,1)}), bf16[64,2,16384]{2,1,0:T(2,128)(2,1)}, u32[]{:S(2)}, u32[]{:S(2)}) async-start(bf16[64,2,16384]{2,1,0:T(2,128)(2,1)} %stack.2), calls=%async_computation | async-start | bytes 8388608 | tf_op jit(solution)/shard_map/all_to_all | solution.py:106
  410.2 181.1 %all-to-all-done = bf16[64,2,16384]{2,1,0:T(2,128)(2,1)} async-done(((bf16[64,2,16384]{2,1,0:T(2,128)(2,1)}), bf16[64,2,16384]{2,1,0:T(2,128)(2,1)}, u32[]{:S(2)}, u32[]{:S(2)}) %all-to-all-start) | async-done | bytes 4194336 | tf_op jit(solution)/shard_map/all_to_all | solution.py:106
  591.3 7.3 %reshape.139 = bf16[128,16384]{1,0:T(8,128)(2,1)} reshape(bf16[64,2,16384]{2,1,0:T(2,128)(2,1)} %all-to-all-done) | data formatting | bytes 8388608 | tf_op jit(solution)/shard_map/reshape | solution.py:106
  598.6 6.0 gather_fusion
  605.1 1.6 bitcast_select_fusion
  (46 shorter events, 4.8 us)
Async XLA Ops:
  7.2 20.7 %copy-start = (f32[1,2,8]{2,1,0:T(2,128)S(1)}, f32[1,2,8]{2,1,0:T(2,128)}, u32[]{:S(2)}) copy-start(f32[1,2,8]{2,1,0:T(2,128)} %param.26) | copy-start | bytes 196
  7.2 4.7 copy-start.2
  7.2 5.3 copy-start.3
  7.2 39.2 %all-gather.5.cloned.1.call-start = ((), (), s32[]{:S(2)}) async-start(), calls=%async_computation.2 | async-start | bytes 2359296 | tf_op jit(solution)/shard_map/all_gather | solution.py:58
  9.2 72.9 %all-gather.3.cloned.1.call-start = ((), (), s32[]{:S(2)}) async-start(), calls=%async_computation.1 | async-start | bytes 2359296 | tf_op jit(solution)/shard_map/all_gather | solution.py:57
  11.1 378.7 %all-reduce.2.cloned.1.call-start = ((), (), s32[]{:S(2)}) async-start(), calls=%async_computation.3 | async-start | bytes 7340032 | tf_op jit(solution)/shard_map/psum | solution.py:93
  12.5 1.3 copy-start.4
  25.6 2.1 copy-start.8
  25.6 2.2 copy-start.9
  25.7 2.4 copy-start.7
  25.7 2.6 copy-start.5
  88.1 3.8 copy-start.1
  100.2 0.9 copy-start.6
  104.8 285.0 %copy-start.10 = (s32[56]{0:T(128)S(1)}, s32[56]{0:T(128)}, u32[]{:S(2)}) copy-start(s32[56]{0:T(128)} %param.23) | copy-start | bytes 676
  400.2 191.1 %all-to-all-start = ((bf16[64,2,16384]{2,1,0:T(2,128)(2,1)}), bf16[64,2,16384]{2,1,0:T(2,128)(2,1)}, u32[]{:S(2)}, u32[]{:S(2)}) async-start(bf16[64,2,16384]{2,1,0:T(2,128)(2,1)} %stack.2), calls=%async_computation | async-start | bytes 8388608 | tf_op jit(solution)/shard_map/all_to_all | solution.py:106
Sparse Core Ops, SparseCore 0:
  10.2 36.2 all-gather.4
  48.6 33.4 all-gather.2
  100.3 289.3 all-reduce.1
